TPU v7x, 32 devices: a whole 2x2x4 slice. The times are simulated.
32 devices in a mesh: gx: 8 (over z, y), gy: 4 (over x, core).
Axes of the slice: x: 2, y: 2, z: 4, core: 2. Of those that a mesh axis runs over, the one named last changes fastest.
Arguments:
- three_index: bfloat16 [8, 4608, 4608], P('gx', 'gy'), as said below
- old_density: bfloat16 [4608, 4608], P('gy'), as said below
- core: float32 [4608, 4608], P('gy', 'gx'), as said below
Outputs:
- purified: bfloat16 [4608, 4608], P('gy', 'gx')
- idempotency: float32 [2], replicated
Inputs may be any that keep to these rules, and one draw needn't show every extreme that they name: Each slab three_index[P] is symmetric in its two basis indices. `old_density`: symmetric. `core`: symmetric.
All inputs are finite; a program needn't handle non-finite values.
Results may differ from a plain program's by a relative error of at most 0.015.
Values may be sent and summed in bfloat16 or wider, within the bound.
A program may use at most 128 MiB of HBM per device.

v0:
```python
import jax
import jax.numpy as jnp
from jax import lax
from jax.sharding import PartitionSpec as P

ITERS = 2


def per_device(three_index, old_density, core):
    aux_dev, rows, width = three_index.shape
    cols = core.shape[1]
    flat = three_index.reshape(aux_dev, rows * width)
    partial_value = jnp.dot(
        flat, old_density.reshape(rows * width), preferred_element_type=jnp.float32
    )
    fitted = lax.psum(partial_value, "gy")
    fitted16 = fitted.astype(jnp.bfloat16)
    coulomb = lax.psum_scatter(
        jnp.einsum("p,prc->cr", fitted16, three_index, preferred_element_type=jnp.float32).astype(
            jnp.bfloat16
        ),
        "gx",
        scatter_dimension=0,
        tiled=True,
    ).astype(jnp.float32)
    fock = core + coulomb.T
    row_start = lax.axis_index("gy") * rows
    col_start = lax.axis_index("gx") * cols
    row_ids = row_start + lax.broadcasted_iota(jnp.int32, (rows, cols), 0)
    col_ids = col_start + lax.broadcasted_iota(jnp.int32, (rows, cols), 1)
    diag_mask = (row_ids == col_ids).astype(jnp.float32)
    local_trace = jnp.sum(fock * diag_mask)
    shift = lax.psum(local_trace, ("gx", "gy")) / width
    shifted = fock - shift * diag_mask
    spread = lax.psum(jnp.sum(shifted * shifted), ("gx", "gy")) / (width * width)
    current = ((shift * diag_mask - fock) / (4.0 * jnp.sqrt(spread + 1e-06))).astype(jnp.bfloat16)
    scale = 1.0 / jnp.sqrt(jnp.float32(width))
    traces = []
    for step in range(ITERS):
        right = lax.all_gather(current, "gy", axis=0, tiled=True)
        row_panel = lax.all_gather(current, "gx", axis=1, tiled=True)
        square_full = jnp.dot(row_panel, right, preferred_element_type=jnp.float32) * scale
        square = square_full.astype(jnp.bfloat16)
        square_block = lax.all_gather(square, "gy", axis=0, tiled=True)
        cube = jnp.dot(row_panel, square_block, preferred_element_type=jnp.float32) * scale
        traces.append(jnp.sum(square_full * diag_mask))
        current = (1.5 * current.astype(jnp.float32) - 2.0 * cube).astype(jnp.bfloat16)
    totals = lax.psum(jnp.stack(traces), ("gx", "gy"))
    idempotency = 16.0 * (0.25 - totals / (width * jnp.sqrt(jnp.float32(width))))
    return (current, idempotency)


def solution(mesh):
    placed = (P("gx", "gy", None), P("gy", None), P("gy", "gx"))
    return jax.shard_map(
        per_device, mesh=mesh, in_specs=placed, out_specs=(P("gy", "gx"), P()), check_vma=False
    )
```

profile of v0, /device:TPU:0, one launch (start us, length us, event | category | flops | bytes accessed | tf_op | source)
XLA Modules:
  0.0 895.6 jit_solution(16187595499375123604)
XLA Ops:
  7.2 0.0 reduce-scatter.2.cloned.1.call-start
  7.2 19.8 %reshape.23 = bf16[5308416]{0:T(1024)(128)(2,1)} reshape(bf16[1,1152,4608]{2,1,0:T(8,128)(2,1)} %param.3) | data formatting | bytes 21233664 | tf_op jit(solution)/shard_map/reshape
  27.0 15.3 %copy.5 = bf16[1,1152,4608]{1,2,0:T(8,128)(2,1)} copy(bf16[1,1152,4608]{2,1,0:T(8,128)(2,1)} %param.3) | data formatting | bytes 21233664 | tf_op args[0]
  42.3 19.8 %reshape.24 = bf16[5308416]{0:T(1024)(128)(2,1)} reshape(bf16[1152,4608]{1,0:T(8,128)(2,1)} %param.4) | data formatting | bytes 21233664 | tf_op jit(solution)/shard_map/reshape | solution.py:14
  62.1 10.9 %fusion = f32[]{:T(128)} fusion(bf16[5308416]{0:T(1024)(128)(2,1)} %reshape.23, bf16[5308416]{0:T(1024)(128)(2,1)} %reshape.24), kind=kLoop, calls=%fused_computation.1 | loop fusion | flops 21233664 | bytes 21233668 | tf_op jit(solution)/shard_map/dot_general | solution.py:13
  72.9 9.0 %psum.28 = bf16[1]{0:T(256)(128)(2,1)} all-reduce(f32[1]{0:T(128)} %bitcast), channel_id=1, replica_groups=mesh['gx'=8,'gy'=4] {'gy'}, use_global_device_ids=true, to_apply=%region_0.0 | all-reduce | flops 1 | bytes 6 | tf_op jit(solution)/shard_map/psum | solution.py:16
  82.6 10.5 %fusion.1 = bf16[4608,1152]{1,0:T(8,128)(2,1)} fusion(bf16[1,1152,4608]{1,2,0:T(8,128)(2,1)} %copy.5, f32[]{:T(128)S(6)} %convert.13), kind=kLoop, calls=%fused_computation.3 | loop fusion | flops 15925248 | bytes 21233668 | tf_op jit(solution)/shard_map/convert_element_type | solution.py:19
  93.1 0.0 copy-start
  93.1 0.0 reduce-scatter.2.cloned.1.call-update
  93.1 0.0 all-gather.9.cloned.1.call-start
  93.2 180.8 %reduce-scatter.2.cloned.1.call-done = bf16[576,1152]{1,0:T(8,128)(2,1)} async-done(((bf16[4608,1152]{1,0:T(8,128)(2,1)}), bf16[576,1152]{1,0:T(8,128)(2,1)}) %reduce-scatter.2.cloned.1.call-update) | async-done | bytes 1327120 | tf_op jit(solution)/shard_map/reduce_scatter | solution.py:18
  274.1 0.0 copy-done
  274.1 2.8 fusion.11
  276.9 39.5 %psum.29 = f32[]{:T(128)} all-reduce(f32[]{:T(128)} %fusion.11), channel_id=1, replica_groups=mesh['gx'=8,'gy'=4] {'gx','gy'}, use_global_device_ids=true, to_apply=%region_3.0 | all-reduce | flops 1 | bytes 8 | tf_op jit(solution)/shard_map/psum | solution.py:33
  317.0 2.9 fusion.10
  319.9 40.2 %psum.30 = f32[]{:T(128)} all-reduce(f32[]{:T(128)} %fusion.10), channel_id=1, replica_groups=mesh['gx'=8,'gy'=4] {'gx','gy'}, use_global_device_ids=true, to_apply=%region_5.0 | all-reduce | flops 1 | bytes 8 | tf_op jit(solution)/shard_map/psum | solution.py:35
  360.8 3.0 fusion.14
  363.8 0.0 all-gather.9.cloned.1.call-update
  363.8 0.0 all-gather.7.cloned.1.call-start
  363.9 0.7 all-gather.7.cloned.1.call-update
  364.6 0.0 copy-start.1
  364.6 0.0 all-gather.11.cloned.1.call-start
  364.6 40.2 %all-gather.9.cloned.1.call-done = bf16[4608,576]{0,1:T(8,128)(2,1)} async-done(((bf16[1152,576]{0,1:T(8,128)(2,1)}), bf16[4608,576]{0,1:T(8,128)(2,1)}) %all-gather.9.cloned.1.call-update) | async-done | bytes 5308432 | tf_op jit(solution)/shard_map/all_gather | solution.py:40
  404.9 154.9 %all-gather.7.cloned.1.call-done = bf16[1152,4608]{0,1:T(8,128)(2,1)} async-done(((bf16[1152,576]{0,1:T(8,128)(2,1)}), bf16[1152,4608]{0,1:T(8,128)(2,1)}) %all-gather.7.cloned.1.call-update) | async-done | bytes 10616848 | tf_op jit(solution)/shard_map/all_gather | solution.py:41
  559.8 13.3 %fusion.15 = (bf16[1152,576]{0,1:T(8,128)(2,1)}, f32[1152,576]{0,1:T(8,128)}) fusion(bf16[4608,576]{0,1:T(8,128)(2,1)} %all-gather.9.cloned.1.call-done, bf16[1152,4608]{0,1:T(8,128)(2,1)} %all-gather.7.cloned.1.call-done), kind=kOutput, calls=%fused_computation.30 | convolution fusion | flops 6116622336 | bytes 19906560 | tf_op jit(solution)/shard_map/dot_general | solution.py:42
  573.1 0.0 all-gather.11.cloned.1.call-update
  573.1 0.2 all-gather.15.cloned.1.call-start
  573.4 38.9 %all-gather.11.cloned.1.call-done = bf16[4608,576]{0,1:T(8,128)(2,1)} async-done(((bf16[1152,576]{0,1:T(8,128)(2,1)}), bf16[4608,576]{0,1:T(8,128)(2,1)}) %all-gather.11.cloned.1.call-update) | async-done | bytes 5308432 | tf_op jit(solution)/shard_map/all_gather | solution.py:44
  612.2 0.0 copy-done.1
  612.2 12.9 %fusion.7 = bf16[1152,576]{0,1:T(8,128)(2,1)} fusion(bf16[4608,576]{0,1:T(8,128)(2,1)} %all-gather.11.cloned.1.call-done, bf16[1152,4608]{0,1:T(8,128)(2,1)} %all-gather.7.cloned.1.call-done, bf16[1152,576]{0,1:T(8,128)(2,1)S(1)} %copy-done.1), kind=kOutput, calls=%fused_computation.17 | convolution fusion | flops 6118612992 | bytes 18579456 | tf_op jit(solution)/shard_map/dot_general | solution.py:45
  625.1 0.0 all-gather.15.cloned.1.call-update
  625.1 0.0 all-gather.13.cloned.1.call-start
  625.2 0.5 all-gather.13.cloned.1.call-update
  625.7 0.0 all-gather.17.cloned.1.call-start
  625.7 40.3 %all-gather.15.cloned.1.call-done = bf16[4608,576]{0,1:T(8,128)(2,1)} async-done(((bf16[1152,576]{0,1:T(8,128)(2,1)}), bf16[4608,576]{0,1:T(8,128)(2,1)}) %all-gather.15.cloned.1.call-update) | async-done | bytes 5308432 | tf_op jit(solution)/shard_map/all_gather | solution.py:40
  666.0 154.8 %all-gather.13.cloned.1.call-done = bf16[1152,4608]{0,1:T(8,128)(2,1)} async-done(((bf16[1152,576]{0,1:T(8,128)(2,1)}), bf16[1152,4608]{0,1:T(8,128)(2,1)}) %all-gather.13.cloned.1.call-update) | async-done | bytes 10616848 | tf_op jit(solution)/shard_map/all_gather | solution.py:41
  820.8 0.0 copy-start.2
  820.8 14.1 %fusion.12 = (f32[]{:T(128)}, f32[]{:T(128)}, bf16[1152,576]{0,1:T(8,128)(2,1)}) fusion(f32[1152,576]{0,1:T(8,128)} %get-tuple-element.6, s32[1152]{0:T(1024)S(1)} %iota_add_fusion, s32[576]{0:T(1024)S(1)} %iota_add_fusion.1, bf16[4608,576]{0,1:T(8,128)(2,1)} %all-gather.15.cloned.1.call-done, bf16[1152,4608]{0,1:T(8,128)(2,1)} %all-gather.13.cloned.1.call-done), kind=kOutput, calls=%fused_computation.22 | convolution fusion | flops 6119940096 | bytes 19913480 | tf_op jit(solution)/shard_map/dot_general | solution.py:42
  834.9 0.0 all-gather.17.cloned.1.call-update
  834.9 1.4 pad_maximum_fusion
  836.3 39.1 %psum.31 = f32[2]{0:T(128)S(1)} all-reduce(f32[2]{0:T(128)S(1)} %pad_maximum_fusion), channel_id=1, replica_groups=mesh['gx'=8,'gy'=4] {'gx','gy'}, use_global_device_ids=true, to_apply=%region_8.0 | all-reduce | flops 2 | bytes 16 | tf_op jit(solution)/shard_map/psum | solution.py:48
  875.4 0.5 subtract_multiply_fusion
  875.9 0.0 all-gather.17.cloned.1.call-done
  875.9 0.0 copy-done.2
  875.9 12.9 %fusion.6 = bf16[1152,576]{0,1:T(8,128)(2,1)} fusion(bf16[4608,576]{0,1:T(8,128)(2,1)} %all-gather.17.cloned.1.call-done, bf16[1152,4608]{0,1:T(8,128)(2,1)} %all-gather.13.cloned.1.call-done, bf16[1152,576]{0,1:T(8,128)(2,1)S(1)} %copy-done.2), kind=kOutput, calls=%fused_computation.16 | convolution fusion | flops 6118612992 | bytes 18579456 | tf_op jit(solution)/shard_map/dot_general | solution.py:45
  (2 shorter events, 0.0 us)
Async XLA Ops:
  7.2 266.9 %reduce-scatter.2.cloned.1.call-start = ((), (), s32[]{:S(2)}) async-start(), calls=%async_computation.1 | async-start | bytes 11943936 | tf_op jit(solution)/shard_map/reduce_scatter | solution.py:18
  93.1 181.0 %copy-start = (f32[1152,576]{0,1:T(8,128)S(1)}, f32[1152,576]{0,1:T(8,128)}, u32[]{:S(2)}) copy-start(f32[1152,576]{0,1:T(8,128)} %param.5) | copy-start | bytes 7962628
  93.1 311.7 %all-gather.9.cloned.1.call-start = ((), (), s32[]{:S(2)}) async-start(), calls=%async_computation.3 | async-start | bytes 6635520 | tf_op jit(solution)/shard_map/all_gather | solution.py:40
  363.8 196.0 %all-gather.7.cloned.1.call-start = ((), (), s32[]{:S(2)}) async-start(), calls=%async_computation.2 | async-start | bytes 11943936 | tf_op jit(solution)/shard_map/all_gather | solution.py:41
  364.6 247.7 %copy-start.1 = (bf16[1152,576]{0,1:T(8,128)(2,1)S(1)}, bf16[1152,576]{0,1:T(8,128)(2,1)}, u32[]{:S(2)}) copy-start(bf16[1152,576]{0,1:T(8,128)(2,1)} %fusion.14) | copy-start | bytes 3981316
  364.6 247.6 %all-gather.11.cloned.1.call-start = ((), (), s32[]{:S(2)}) async-start(), calls=%async_computation.4 | async-start | bytes 6635520 | tf_op jit(solution)/shard_map/all_gather | solution.py:44
  573.1 92.9 %all-gather.15.cloned.1.call-start = ((), (), s32[]{:S(2)}) async-start(), calls=%async_computation.6 | async-start | bytes 6635520 | tf_op jit(solution)/shard_map/all_gather | solution.py:40
  625.1 195.7 %all-gather.13.cloned.1.call-start = ((), (), s32[]{:S(2)}) async-start(), calls=%async_computation.5 | async-start | bytes 11943936 | tf_op jit(solution)/shard_map/all_gather | solution.py:41
  625.7 250.2 %all-gather.17.cloned.1.call-start = ((), (), s32[]{:S(2)}) async-start(), calls=%async_computation.7 | async-start | bytes 6635520 | tf_op jit(solution)/shard_map/all_gather | solution.py:44
  820.8 55.1 %copy-start.2 = (bf16[1152,576]{0,1:T(8,128)(2,1)S(1)}, bf16[1152,576]{0,1:T(8,128)(2,1)}, u32[]{:S(2)}) copy-start(bf16[1152,576]{0,1:T(8,128)(2,1)} %fusion.7) | copy-start | bytes 3981316
Sparse Core Ops, SparseCore 0:
  93.3 180.7 reduce-scatter.1
  363.9 40.8 all-gather.8
  407.6 152.1 all-gather.6
  573.3 38.9 all-gather.10
  625.2 40.7 all-gather.14
  668.6 152.1 all-gather.12
  835.0 39.4 all-gather.16
where the time goes:
time: 897 us; the launch traced here: 896 us
  waiting for transfers between devices  611 us (68%)
  blocking collectives  128 us (14%)
  local copies, waits for them, and re-layouts  54.9 us (6%)
  matrix products  53.1 us (6%)
  other arithmetic  32 us (4%)
  between operations  16.2 us (2%)
    all_gather x2, waiting for transfers between devices, per_device(): row_panel = lax.all_gather(current, 'gx', axis=1, tiled=True)  310 us
    reduce_scatter x1, waiting for transfers between devices, per_device(): lax.psum_scatter(jnp.einsum('p,prc->cr', fitted16, three_index, preferred...  181 us
    all_gather x2, waiting for transfers between devices, per_device(): right = lax.all_gather(current, 'gy', axis=0, tiled=True)  80.5 us
    psum x1, blocking collectives, per_device(): lax.psum(jnp.sum(shifted * shifted), ('gx', 'gy')) / (width * width)  40.2 us
    psum x1, blocking collectives, per_device(): shift = lax.psum(local_trace, ('gx', 'gy')) / width  39.5 us
    psum x1, blocking collectives, per_device(): totals = lax.psum(jnp.stack(traces), ('gx', 'gy'))  39.1 us
    all_gather x2, waiting for transfers between devices, per_device(): square_block = lax.all_gather(square, 'gy', axis=0, tiled=True)  38.9 us
    dot_general x2, matrix products, per_device(): jnp.dot(row_panel, right, preferred_element_type=jnp.float32) * scale  27.4 us
  transfers between devices with their start and end apart: 7, of which 6 were waited for; matrix products, arithmetic and copies ran while one was open for 0% of the time, Pallas kernels for 0%

commit v1 on v0

--- a/solution.py
+++ b/solution.py
@@ -4,6 +4,21 @@
 from jax.sharding import PartitionSpec as P
 
 ITERS = 2
+
+
+def area_supply(in_array):
+    axis_id = "gy"
+    world = lax.axis_size(axis_id)
+    upper = [(tick - 1, tick) for tick in range(1, world)] + [(world - 1, 0)]
+    raw_out = in_array
+    dev = 0
+    by_rank = [raw_out]
+    while dev < world - 1:
+        raw_out = lax.ppermute(raw_out, axis_id, upper)
+        by_rank += [raw_out]
+        dev = dev + 1
+    near = jnp.concatenate([*reversed(by_rank)], 0)
+    return jnp.roll(near, (lax.axis_index(axis_id) + 1) * raw_out.shape[0], 0)
 
 
 def per_device(three_index, old_density, core):
@@ -37,7 +52,7 @@
     scale = 1.0 / jnp.sqrt(jnp.float32(width))
     traces = []
     for step in range(ITERS):
-        right = lax.all_gather(current, "gy", axis=0, tiled=True)
+        right = area_supply(current)
         row_panel = lax.all_gather(current, "gx", axis=1, tiled=True)
         square_full = jnp.dot(row_panel, right, preferred_element_type=jnp.float32) * scale
         square = square_full.astype(jnp.bfloat16)

time: 897 us -> 834 us (0.930)
  waiting for transfers between devices: 611 us -> 523 us
  matrix products: 53.1 us -> 77.4 us
    all_gather x2, waiting for transfers between devices: 310 us -> 199 us  [per_device(): row_panel = lax.all_gather(current, 'gx', axis=1, tiled=True)]
    ppermute x0 -> x6, waiting for transfers between devices: none -> 104 us  [area_supply(): raw_out = lax.ppermute(raw_out, axis_id, upper)]
    all_gather x2 -> x0, waiting for transfers between devices: 80.5 us -> none  [per_device(): right = lax.all_gather(current, 'gy', axis=0, tiled=True)]
    dot_general x2, matrix products: 27.4 us -> 51.6 us  [per_device(): jnp.dot(row_panel, right, preferred_element_type=jnp.float32) * scale]
  transfers between devices with their start and end apart: 7 -> 11, of which waited for: 6 -> 10; matrix products, arithmetic and copies ran while one was open for 0% -> 0% of each run, Pallas kernels for 0% -> 0%
where the time goes in v1:
time: 834 us; the launch traced here: 833 us
  waiting for transfers between devices  523 us (63%)
  blocking collectives  128 us (15%)
  matrix products  77.4 us (9%)
  local copies, waits for them, and re-layouts  56 us (7%)
  other arithmetic  32 us (4%)
  between operations  15.8 us (2%)
    all_gather x2, waiting for transfers between devices, per_device(): row_panel = lax.all_gather(current, 'gx', axis=1, tiled=True)  199 us
    reduce_scatter x1, waiting for transfers between devices, per_device(): lax.psum_scatter(jnp.einsum('p,prc->cr', fitted16, three_index, preferred...  181 us
    ppermute x6, waiting for transfers between devices, area_supply(): raw_out = lax.ppermute(raw_out, axis_id, upper)  104 us
    dot_general x2, matrix products, per_device(): jnp.dot(row_panel, right, preferred_element_type=jnp.float32) * scale  51.6 us
    psum x1, blocking collectives, per_device(): lax.psum(jnp.sum(shifted * shifted), ('gx', 'gy')) / (width * width)  40.2 us
    psum x1, blocking collectives, per_device(): shift = lax.psum(local_trace, ('gx', 'gy')) / width  39.5 us
    psum x1, blocking collectives, per_device(): totals = lax.psum(jnp.stack(traces), ('gx', 'gy'))  39.1 us
    all_gather x2, waiting for transfers between devices, per_device(): square_block = lax.all_gather(square, 'gy', axis=0, tiled=True)  39 us
  transfers between devices with their start and end apart: 11, of which 10 were waited for; matrix products, arithmetic and copies ran while one was open for 0% of the time, Pallas kernels for 0%

profile of v1, /device:TPU:0, one launch (start us, length us, event | category | flops | bytes accessed | tf_op | source)
XLA Modules:
  0.0 832.6 jit_solution(9731788551176552678)
XLA Ops:
  7.2 0.0 reduce-scatter.2.cloned.1.call-start
  7.2 19.8 %reshape.23 = bf16[5308416]{0:T(1024)(128)(2,1)} reshape(bf16[1,1152,4608]{2,1,0:T(8,128)(2,1)} %param.5) | data formatting | bytes 21233664 | tf_op jit(solution)/shard_map/reshape
  27.0 15.3 %copy.5 = bf16[1,1152,4608]{1,2,0:T(8,128)(2,1)} copy(bf16[1,1152,4608]{2,1,0:T(8,128)(2,1)} %param.5) | data formatting | bytes 21233664 | tf_op args[0]
  42.3 19.8 %reshape.24 = bf16[5308416]{0:T(1024)(128)(2,1)} reshape(bf16[1152,4608]{1,0:T(8,128)(2,1)} %param.6) | data formatting | bytes 21233664 | tf_op jit(solution)/shard_map/reshape | solution.py:29
  62.1 10.9 %fusion = f32[]{:T(128)} fusion(bf16[5308416]{0:T(1024)(128)(2,1)} %reshape.23, bf16[5308416]{0:T(1024)(128)(2,1)} %reshape.24), kind=kLoop, calls=%fused_computation.1 | loop fusion | flops 21233664 | bytes 21233668 | tf_op jit(solution)/shard_map/dot_general | solution.py:28
  72.9 9.0 %psum.28 = bf16[1]{0:T(256)(128)(2,1)} all-reduce(f32[1]{0:T(128)} %bitcast), channel_id=1, replica_groups=mesh['gx'=8,'gy'=4] {'gy'}, use_global_device_ids=true, to_apply=%region_0.0 | all-reduce | flops 1 | bytes 6 | tf_op jit(solution)/shard_map/psum | solution.py:31
  82.6 10.5 %fusion.1 = bf16[4608,1152]{1,0:T(8,128)(2,1)} fusion(bf16[1,1152,4608]{1,2,0:T(8,128)(2,1)} %copy.5, f32[]{:T(128)S(6)} %convert.13), kind=kLoop, calls=%fused_computation.3 | loop fusion | flops 15925248 | bytes 21233668 | tf_op jit(solution)/shard_map/convert_element_type | solution.py:34
  93.1 0.0 copy-start
  93.1 0.0 reduce-scatter.2.cloned.1.call-update
  93.1 0.0 all-gather.5.cloned.1.call-start
  93.2 180.8 %reduce-scatter.2.cloned.1.call-done = bf16[576,1152]{1,0:T(8,128)(2,1)} async-done(((bf16[4608,1152]{1,0:T(8,128)(2,1)}), bf16[576,1152]{1,0:T(8,128)(2,1)}) %reduce-scatter.2.cloned.1.call-update) | async-done | bytes 1327120 | tf_op jit(solution)/shard_map/reduce_scatter | solution.py:33
  274.1 0.0 copy-done
  274.1 2.8 fusion.37
  276.9 39.5 %psum.29 = f32[]{:T(128)} all-reduce(f32[]{:T(128)} %fusion.37), channel_id=1, replica_groups=mesh['gx'=8,'gy'=4] {'gx','gy'}, use_global_device_ids=true, to_apply=%region_3.0 | all-reduce | flops 1 | bytes 8 | tf_op jit(solution)/shard_map/psum | solution.py:48
  317.0 2.9 fusion.36
  319.9 40.2 %psum.30 = f32[]{:T(128)} all-reduce(f32[]{:T(128)} %fusion.36), channel_id=1, replica_groups=mesh['gx'=8,'gy'=4] {'gx','gy'}, use_global_device_ids=true, to_apply=%region_5.0 | all-reduce | flops 1 | bytes 8 | tf_op jit(solution)/shard_map/psum | solution.py:50
  360.8 3.0 fusion.40
  363.8 0.0 all-gather.5.cloned.1.call-update
  363.8 0.0 all-gather.7.cloned.1.call-start
  363.9 0.1 collective-permute-start
  364.0 17.4 %collective-permute-done = bf16[1152,576]{0,1:T(8,128)(2,1)S(1)} collective-permute-done((bf16[1152,576]{0,1:T(8,128)(2,1)}, bf16[1152,576]{0,1:T(8,128)(2,1)S(1)}, u32[]{:S(2)}, u32[]{:S(2)}) %collective-permute-start) | collective-permute-done | bytes 1327136 | tf_op jit(solution)/shard_map/ppermute | solution.py:17
  381.4 0.0 collective-permute-start.1
  381.4 17.3 %collective-permute-done.1 = bf16[1152,576]{0,1:T(8,128)(2,1)} collective-permute-done((bf16[1152,576]{0,1:T(8,128)(2,1)S(1)}, bf16[1152,576]{0,1:T(8,128)(2,1)}, u32[]{:S(2)}, u32[]{:S(2)}) %collective-permute-start.1) | collective-permute-done | bytes 1327136 | tf_op jit(solution)/shard_map/ppermute | solution.py:17
  398.7 0.0 collective-permute-start.2
  398.7 0.0 copy-start.1
  398.7 17.5 %collective-permute-done.2 = bf16[1152,576]{0,1:T(8,128)(2,1)} collective-permute-done((bf16[1152,576]{0,1:T(8,128)(2,1)}, bf16[1152,576]{0,1:T(8,128)(2,1)}, u32[]{:S(2)}, u32[]{:S(2)}) %collective-permute-start.2) | collective-permute-done | bytes 1327136 | tf_op jit(solution)/shard_map/ppermute | solution.py:17
  416.2 100.0 %all-gather.5.cloned.1.call-done = bf16[1152,4608]{0,1:T(8,128)(2,1)} async-done(((bf16[1152,576]{0,1:T(8,128)(2,1)}), bf16[1152,4608]{0,1:T(8,128)(2,1)}) %all-gather.5.cloned.1.call-update) | async-done | bytes 10616848 | tf_op jit(solution)/shard_map/all_gather | solution.py:56
  516.2 25.3 %fusion.45 = (bf16[1152,576]{0,1:T(8,128)(2,1)}, f32[1152,576]{0,1:T(8,128)}) fusion(bf16[1152,4608]{0,1:T(8,128)(2,1)} %all-gather.5.cloned.1.call-done, s32[]{:T(128)S(6)} %select_n.13, bf16[1152,576]{0,1:T(8,128)(2,1)} %collective-permute-done.2, bf16[1152,576]{0,1:T(8,128)(2,1)} %collective-permute-done.1, ...), kind=kOutput, calls=%fused_computation.66 | convolution fusion | flops 6159089664 | bytes 19906564 | tf_op jit(solution)/shard_map/dot_general | solution.py:57
  541.5 0.0 all-gather.7.cloned.1.call-update
  541.5 0.0 all-gather.9.cloned.1.call-start
  541.6 39.0 %all-gather.7.cloned.1.call-done = bf16[4608,576]{0,1:T(8,128)(2,1)} async-done(((bf16[1152,576]{0,1:T(8,128)(2,1)}), bf16[4608,576]{0,1:T(8,128)(2,1)}) %all-gather.7.cloned.1.call-update) | async-done | bytes 5308432 | tf_op jit(solution)/shard_map/all_gather | solution.py:59
  580.6 0.0 copy-done.1
  580.6 12.9 %fusion.33 = bf16[1152,576]{0,1:T(8,128)(2,1)} fusion(bf16[4608,576]{0,1:T(8,128)(2,1)} %all-gather.7.cloned.1.call-done, bf16[1152,4608]{0,1:T(8,128)(2,1)} %all-gather.5.cloned.1.call-done, bf16[1152,576]{0,1:T(8,128)(2,1)S(1)} %copy-done.1), kind=kOutput, calls=%fused_computation.49 | convolution fusion | flops 6118612992 | bytes 18579456 | tf_op jit(solution)/shard_map/dot_general | solution.py:60
  593.5 0.0 all-gather.9.cloned.1.call-update
  593.5 0.0 all-gather.11.cloned.1.call-start
  593.5 0.3 collective-permute-start.3
  593.8 17.2 %collective-permute-done.3 = bf16[1152,576]{0,1:T(8,128)(2,1)S(1)} collective-permute-done((bf16[1152,576]{0,1:T(8,128)(2,1)}, bf16[1152,576]{0,1:T(8,128)(2,1)S(1)}, u32[]{:S(2)}, u32[]{:S(2)}) %collective-permute-start.3) | collective-permute-done | bytes 1327136 | tf_op jit(solution)/shard_map/ppermute | solution.py:17
  611.0 0.0 collective-permute-start.4
  611.0 17.2 %collective-permute-done.4 = bf16[1152,576]{0,1:T(8,128)(2,1)S(1)} collective-permute-done((bf16[1152,576]{0,1:T(8,128)(2,1)S(1)}, bf16[1152,576]{0,1:T(8,128)(2,1)S(1)}, u32[]{:S(2)}, u32[]{:S(2)}) %collective-permute-start.4) | collective-permute-done | bytes 1327136 | tf_op jit(solution)/shard_map/ppermute | solution.py:17
  628.2 0.0 copy-start.3
  628.2 1.1 copy-done.3
  629.3 0.0 collective-permute-start.5
  629.3 17.3 %collective-permute-done.5 = bf16[1152,576]{0,1:T(8,128)(2,1)} collective-permute-done((bf16[1152,576]{0,1:T(8,128)(2,1)S(1)}, bf16[1152,576]{0,1:T(8,128)(2,1)}, u32[]{:S(2)}, u32[]{:S(2)}) %collective-permute-start.5) | collective-permute-done | bytes 1327136 | tf_op jit(solution)/shard_map/ppermute | solution.py:17
  646.7 99.1 %all-gather.9.cloned.1.call-done = bf16[1152,4608]{0,1:T(8,128)(2,1)} async-done(((bf16[1152,576]{0,1:T(8,128)(2,1)}), bf16[1152,4608]{0,1:T(8,128)(2,1)}) %all-gather.9.cloned.1.call-update) | async-done | bytes 10616848 | tf_op jit(solution)/shard_map/all_gather | solution.py:56
  745.8 0.0 copy-start.2
  745.8 26.4 %fusion.38 = (f32[]{:T(128)}, f32[]{:T(128)}, bf16[1152,576]{0,1:T(8,128)(2,1)}) fusion(f32[1152,576]{0,1:T(8,128)} %get-tuple-element.7, s32[1152]{0:T(1024)S(1)} %iota_add_fusion, s32[576]{0:T(1024)S(1)} %iota_add_fusion.1, bf16[1152,4608]{0,1:T(8,128)(2,1)} %all-gather.9.cloned.1.call-done, s32[]{:T(128)S(6)} %select_n.13, ...), kind=kOutput, calls=%fused_computation.54 | convolution fusion | flops 6162407424 | bytes 19913484 | tf_op jit(solution)/shard_map/dot_general | solution.py:57
  772.1 0.0 all-gather.11.cloned.1.call-update
  772.2 1.4 pad_maximum_fusion
  773.6 39.1 %psum.31 = f32[2]{0:T(128)S(1)} all-reduce(f32[2]{0:T(128)S(1)} %pad_maximum_fusion), channel_id=1, replica_groups=mesh['gx'=8,'gy'=4] {'gx','gy'}, use_global_device_ids=true, to_apply=%region_8.10 | all-reduce | flops 2 | bytes 16 | tf_op jit(solution)/shard_map/psum | solution.py:63
  812.7 0.5 subtract_multiply_fusion
  813.2 0.0 all-gather.11.cloned.1.call-done
  813.2 0.0 copy-done.2
  813.2 12.9 %fusion.32 = bf16[1152,576]{0,1:T(8,128)(2,1)} fusion(bf16[4608,576]{0,1:T(8,128)(2,1)} %all-gather.11.cloned.1.call-done, bf16[1152,4608]{0,1:T(8,128)(2,1)} %all-gather.9.cloned.1.call-done, bf16[1152,576]{0,1:T(8,128)(2,1)S(1)} %copy-done.2), kind=kOutput, calls=%fused_computation.48 | convolution fusion | flops 6118612992 | bytes 18579456 | tf_op jit(solution)/shard_map/dot_general | solution.py:60
  (2 shorter events, 0.0 us)
Async XLA Ops:
  7.2 266.9 %reduce-scatter.2.cloned.1.call-start = ((), (), s32[]{:S(2)}) async-start(), calls=%async_computation.1 | async-start | bytes 11943936 | tf_op jit(solution)/shard_map/reduce_scatter | solution.py:33
  93.1 181.0 %copy-start = (f32[1152,576]{0,1:T(8,128)S(1)}, f32[1152,576]{0,1:T(8,128)}, u32[]{:S(2)}) copy-start(f32[1152,576]{0,1:T(8,128)} %param.7) | copy-start | bytes 7962628
  93.1 423.1 %all-gather.5.cloned.1.call-start = ((), (), s32[]{:S(2)}) async-start(), calls=%async_computation.2 | async-start | bytes 11943936 | tf_op jit(solution)/shard_map/all_gather | solution.py:56
  363.8 216.8 %all-gather.7.cloned.1.call-start = ((), (), s32[]{:S(2)}) async-start(), calls=%async_computation.3 | async-start | bytes 6635520 | tf_op jit(solution)/shard_map/all_gather | solution.py:59
  363.9 17.5 %collective-permute-start = (bf16[1152,576]{0,1:T(8,128)(2,1)}, bf16[1152,576]{0,1:T(8,128)(2,1)S(1)}, u32[]{:S(2)}, u32[]{:S(2)}) collective-permute-start(bf16[1152,576]{0,1:T(8,128)(2,1)} %fusion.40), channel_id=1, source_target_pairs={{0,1},{1,2},{2,3},{3,0},{4,5},{5,6},{6,7},{7,4},{8,9},{9,10},{10,1... | collective-permute-start | bytes 3981320 | tf_op jit(solution)/shard_map/ppermute | solution.py:17
  381.4 17.3 %collective-permute-start.1 = (bf16[1152,576]{0,1:T(8,128)(2,1)S(1)}, bf16[1152,576]{0,1:T(8,128)(2,1)}, u32[]{:S(2)}, u32[]{:S(2)}) collective-permute-start(bf16[1152,576]{0,1:T(8,128)(2,1)S(1)} %collective-permute-done), channel_id=1, source_target_pairs={{0,1},{1,2},{2,3},{3,0},{4,5},{5,6},{6,7},{7,4},{8,9},{9,10},{10,1... | collective-permute-start | bytes 3981320 | tf_op jit(solution)/shard_map/ppermute | solution.py:17
  398.7 17.5 %collective-permute-start.2 = (bf16[1152,576]{0,1:T(8,128)(2,1)}, bf16[1152,576]{0,1:T(8,128)(2,1)}, u32[]{:S(2)}, u32[]{:S(2)}) collective-permute-start(bf16[1152,576]{0,1:T(8,128)(2,1)} %collective-permute-done.1), channel_id=1, source_target_pairs={{0,1},{1,2},{2,3},{3,0},{4,5},{5,6},{6,7},{7,4},{8,9},{9,10},{10,1... | collective-permute-start | bytes 3981320 | tf_op jit(solution)/shard_map/ppermute | solution.py:17
  398.7 181.9 %copy-start.1 = (bf16[1152,576]{0,1:T(8,128)(2,1)S(1)}, bf16[1152,576]{0,1:T(8,128)(2,1)}, u32[]{:S(2)}) copy-start(bf16[1152,576]{0,1:T(8,128)(2,1)} %fusion.40) | copy-start | bytes 3981316
  541.5 204.2 %all-gather.9.cloned.1.call-start = ((), (), s32[]{:S(2)}) async-start(), calls=%async_computation.4 | async-start | bytes 11943936 | tf_op jit(solution)/shard_map/all_gather | solution.py:56
  593.5 219.7 %all-gather.11.cloned.1.call-start = ((), (), s32[]{:S(2)}) async-start(), calls=%async_computation.5 | async-start | bytes 6635520 | tf_op jit(solution)/shard_map/all_gather | solution.py:59
  593.5 17.5 %collective-permute-start.3 = (bf16[1152,576]{0,1:T(8,128)(2,1)}, bf16[1152,576]{0,1:T(8,128)(2,1)S(1)}, u32[]{:S(2)}, u32[]{:S(2)}) collective-permute-start(bf16[1152,576]{0,1:T(8,128)(2,1)} %fusion.33), channel_id=1, source_target_pairs={{0,1},{1,2},{2,3},{3,0},{4,5},{5,6},{6,7},{7,4},{8,9},{9,10},{10,1... | collective-permute-start | bytes 3981320 | tf_op jit(solution)/shard_map/ppermute | solution.py:17
  611.0 17.2 %collective-permute-start.4 = (bf16[1152,576]{0,1:T(8,128)(2,1)S(1)}, bf16[1152,576]{0,1:T(8,128)(2,1)S(1)}, u32[]{:S(2)}, u32[]{:S(2)}) collective-permute-start(bf16[1152,576]{0,1:T(8,128)(2,1)S(1)} %collective-permute-done.3), channel_id=1, source_target_pairs={{0,1},{1,2},{2,3},{3,0},{4,5},{5,6},{6,7},{7,4},{8,9},{9,10},{10,1... | collective-permute-start | bytes 3981320 | tf_op jit(solution)/shard_map/ppermute | solution.py:17
  628.2 1.1 copy-start.3
  629.3 17.3 %collective-permute-start.5 = (bf16[1152,576]{0,1:T(8,128)(2,1)S(1)}, bf16[1152,576]{0,1:T(8,128)(2,1)}, u32[]{:S(2)}, u32[]{:S(2)}) collective-permute-start(bf16[1152,576]{0,1:T(8,128)(2,1)S(1)} %collective-permute-done.4), channel_id=1, source_target_pairs={{0,1},{1,2},{2,3},{3,0},{4,5},{5,6},{6,7},{7,4},{8,9},{9,10},{10,1... | collective-permute-start | bytes 3981320 | tf_op jit(solution)/shard_map/ppermute | solution.py:17
  745.8 67.4 %copy-start.2 = (bf16[1152,576]{0,1:T(8,128)(2,1)S(1)}, bf16[1152,576]{0,1:T(8,128)(2,1)}, u32[]{:S(2)}) copy-start(bf16[1152,576]{0,1:T(8,128)(2,1)} %fusion.33) | copy-start | bytes 3981316
Sparse Core Ops, SparseCore 0:
  93.3 180.7 reduce-scatter.1
  364.0 152.2 all-gather.4
  541.7 38.8 all-gather.6
  593.6 152.1 all-gather.8
  772.3 39.4 all-gather.10
